TPU v7x, 8 devices: a whole 2x2x1 slice. The times are simulated.
8 devices in a mesh: dp: 2 (over z, y), tp: 4 (over x, core).
Axes of the slice: x: 2, y: 2, z: 1, core: 2. Of those that a mesh axis runs over, the one named last changes fastest.
Arguments:
- query: bfloat16 [128, 28, 128], P('dp', 'tp'), parts along dimension 0
- k_cache: bfloat16 [128, 2048, 4, 128], P('dp', None, 'tp'), parts along dimension 0
- v_cache: bfloat16 [128, 2048, 4, 128], P('dp', None, 'tp'), parts along dimension 0
- k_new: bfloat16 [128, 4, 128], P('dp', 'tp'), parts along dimension 0
- v_new: bfloat16 [128, 4, 128], P('dp', 'tp'), parts along dimension 0
- lens: int32 [128], P('dp'), parts along dimension 0
Outputs:
- output 1: bfloat16 [128, 28, 128], P('dp', 'tp'), parts along dimension 0
- output 2: bfloat16 [128, 2048, 4, 128], P('dp', 'tp'), parts along dimension 0
- output 3: bfloat16 [128, 2048, 4, 128], P('dp', 'tp'), parts along dimension 0
There are 2 independent parts. A program takes and returns all parts, laid end to end along the dimension named above; each array names one.
All inputs are finite; a program needn't handle non-finite values.
Results may differ from a plain program's by a relative error of at most 0.00775914.
Values are sent between devices in bfloat16 or wider.
A program may use at most 1 GiB of HBM per device.

v0:
```python
import functools

import jax
import jax.numpy as jnp
from jax import lax
from jax.experimental import pallas as pl
from jax.experimental.pallas import tpu as pltpu
from jax.sharding import PartitionSpec as P


FIRST = (63, 1, 1)
CHUNKS = ((0, 4, 4), (4, 36, 4), (40, 20, 4), (60, 2, 2))
LAST = (62, 2, 2)
LAST_SPLIT = (11, 5)
LAST_AFTER = 2
PEERS = (2, 3, 1)
FIRST_PEERS = (PEERS[:1], PEERS[1:])
ROWS = 16
ANY = pl.BlockSpec(memory_space=pl.ANY)


def put_row(ref, index, slot, row):
    @pl.when((slot >= 0) & (slot < ref.shape[-2]))
    def _():
        base = pl.multiple_of((slot // ROWS) * ROWS, ROWS)
        window = (*index, pl.ds(base, ROWS), slice(None))
        old = ref[window].astype(jnp.float32)
        at = lax.broadcasted_iota(jnp.int32, old.shape, 0) == slot - base
        ref[window] = jnp.where(at, row, old).astype(ref.dtype)


def first_kernel(req, size, seq_part, peers, lens_hbm, k_hbm, v_hbm, k_new_hbm, v_new_hbm, *refs):
    outs, (lens, new_rows, sems) = refs[: len(peers)], refs[len(peers) :]
    me = lax.axis_index("tp")
    base = req // ROWS * ROWS
    copies = [pltpu.make_async_copy(lens_hbm, lens, sems.at[0])]
    for t, (cache, new) in enumerate(((k_hbm, k_new_hbm), (v_hbm, v_new_hbm))):
        copies.append(pltpu.make_async_copy(new.at[pl.ds(base, ROWS)], new_rows.at[t], sems.at[1 + t]))
        for i, x in enumerate(peers):
            piece = cache.at[pl.ds(req, size), pl.ds((me ^ x) * seq_part, seq_part)]
            copies.append(pltpu.make_async_copy(piece, outs[i].at[t], sems.at[3 + t * len(peers) + i]))
    for copy in copies:
        copy.start()
    for copy in copies:
        copy.wait()
    for t in range(2):
        for r in range(size):
            row = new_rows[t, pl.ds(req + r - base, 1), :].astype(jnp.float32)
            for i, x in enumerate(peers):
                put_row(outs[i], (t, r), lens[req + r] - (me ^ x) * seq_part, row)


def first_pieces(lens, k_cache, v_cache, k_new, v_new, chunk, peers, make, seq_part):
    first, size, _ = chunk
    head_dim = k_new.shape[-1]
    count = len(peers)
    return pl.pallas_call(
        functools.partial(first_kernel, first, size, seq_part, peers),
        out_shape=[make((2, size, seq_part, head_dim), jnp.bfloat16)] * count,
        in_specs=[ANY] * 5,
        out_specs=[pl.BlockSpec(memory_space=pltpu.VMEM)] * count,
        scratch_shapes=[pltpu.SMEM(lens.shape, jnp.int32), pltpu.VMEM((2, ROWS, head_dim), jnp.bfloat16), pltpu.SemaphoreType.DMA((3 + 2 * count,))],
    )(lens, k_cache, v_cache, k_new, v_new)


def attend_kernel(first, group, seq_part, parts, n_skip, lens_ref, q_ref, k_ref, v_ref, k_new_ref, v_new_ref, *refs):
    (out_ref, *pieces), (k_rows, v_rows) = refs[n_skip:-2], refs[-2:]
    me = lax.axis_index("tp")
    k_rows[...] = k_new_ref[...].astype(jnp.float32)
    v_rows[...] = v_new_ref[...].astype(jnp.float32)
    dims = (((1,), (1,)), ((), ()))
    for r in range(group):
        req = first + pl.program_id(0) * group + r
        length = lens_ref[req]
        for t, (cache, new) in enumerate(((k_ref, k_rows), (v_ref, v_rows))):
            for piece, (x, row0) in zip(pieces, parts):
                if r >= piece.shape[1]:
                    continue
                start = pl.multiple_of((me ^ x) * seq_part + row0, ROWS)
                piece[t, r] = cache[r, pl.ds(start, piece.shape[2]), :]
                put_row(piece, (t, r), length - start, new[pl.ds(req, 1), :])
        query = q_ref[r]
        scale = query.shape[-1] ** -0.5
        scores = lax.dot_general(query, k_ref[r], dims, preferred_element_type=jnp.float32) * scale
        valid = lax.broadcasted_iota(jnp.int32, scores.shape, 1) < length
        scores = jnp.where(valid, scores, -jnp.inf)
        new_score = jnp.sum(query.astype(jnp.float32) * k_rows[pl.ds(req, 1), :], axis=-1, keepdims=True) * scale
        top = jnp.maximum(jnp.max(scores, axis=-1, keepdims=True), new_score)
        weights = jnp.exp(scores - top)
        new_weight = jnp.exp(new_score - top)
        total = jnp.sum(weights, axis=-1, keepdims=True) + new_weight
        probs = (weights / total).astype(jnp.bfloat16)
        new_prob = (new_weight / total).astype(jnp.bfloat16).astype(jnp.float32)
        out = jnp.dot(probs, v_ref[r], preferred_element_type=jnp.float32) + new_prob * v_rows[pl.ds(req, 1), :]
        out_ref[r] = out.astype(jnp.bfloat16)


def attend(lens, query, k_cache, v_cache, k_new, v_new, chunk, ranges, seq_part, n_own=0, buf=(), after=(), sent=0):
    first, size, group = chunk[0] - sent, chunk[1] + sent, chunk[2]
    batch, seq_len, head_dim = k_cache.shape
    rows = query.shape[1]
    parts = [(x, row0, n) for row0, n in ranges for x in PEERS + (0,) * (n_own > 0)]
    at = lambda i, lens: (first // group + i, 0, 0)
    cache = pl.BlockSpec((group, seq_len, head_dim), at)
    heads = pl.BlockSpec((group, rows, head_dim), at)
    whole = pl.BlockSpec((batch, head_dim), lambda i, lens: (0, 0))
    piece = lambda x, n: pl.BlockSpec((2, n_own or group, n, head_dim), lambda i, lens: (0, jnp.maximum(i - sent // group, 0), 0, 0)) if x else pl.BlockSpec(memory_space=pltpu.VMEM)
    shape = lambda x, n: (jax.ShapeDtypeStruct if x else pltpu.VMEM)((2, n_own or size - sent, n, head_dim), jnp.bfloat16)
    return pl.pallas_call(
        functools.partial(attend_kernel, first, group, seq_part, [p[:2] for p in parts], len(buf) + len(after)),
        out_shape=[jax.ShapeDtypeStruct(query.shape, jnp.bfloat16)] + [shape(x, n) for x, _, n in parts],
        grid_spec=pltpu.PrefetchScalarGridSpec(
            num_scalar_prefetch=1,
            grid=(size // group,),
            in_specs=[heads, cache, cache, whole, whole] + [ANY] * (len(buf) + len(after)),
            out_specs=[heads] + [piece(x, n) for x, _, n in parts],
            scratch_shapes=[pltpu.VMEM((batch, head_dim), jnp.float32)] * 2,
        ),
        input_output_aliases={6: 0} if buf else {},
        cost_estimate=pl.CostEstimate(flops=10**6 * size, bytes_accessed=size * seq_len * head_dim * 7, transcendentals=0),
    )(lens, query, k_cache, v_cache, k_new, v_new, *buf, *after)


def interleave_kernel(chunk, n_skip, me_ref, lens_ref, *refs):
    first, _, group = chunk
    count = len(PEERS)
    heads = count + 1
    owns, pieces, new_refs = refs[:2], refs[2 : 2 + count], refs[2 + count : 4 + count]
    outs, (mixed, new_rows) = refs[4 + count + n_skip : 6 + count + n_skip], refs[6 + count + n_skip :]
    me = me_ref[0]
    rows = owns[0].shape[1]

    @pl.loop(0, group)
    def _(r):
        req = first + pl.program_id(0) * group + r
        slot = lens_ref[req] - me * rows
        for t in range(2):
            mixed[pl.ds(me, rows, heads), :] = owns[t][r].astype(jnp.float32)
            for i, x in enumerate(PEERS):
                mixed[pl.ds(me ^ x, rows, heads), :] = pieces[i][t, r].astype(jnp.float32)

            @pl.when((slot >= 0) & (slot < rows))
            def _():
                new_rows[...] = new_refs[t][...].astype(jnp.float32)
                mixed[pl.ds(slot * heads + me, 1), :] = new_rows[pl.ds(req, 1), :]

            outs[t][r] = mixed[...].astype(jnp.bfloat16)


def interleave(me, lens, k_cache, v_cache, pieces, k_new, v_new, bufs, chunk, seq_part):
    first, size, group = chunk
    batch, head_dim = k_new.shape
    heads = len(PEERS) + 1
    own = pl.BlockSpec((group, seq_part, head_dim), lambda i, me, lens: (first // group + i, me[0], 0))
    piece = pl.BlockSpec((2, group, seq_part, head_dim), lambda i, me, lens: (0, i, 0, 0))
    whole = pl.BlockSpec((batch, head_dim), lambda i, me, lens: (0, 0))
    out = pl.BlockSpec((group, seq_part * heads, head_dim), lambda i, me, lens: (first // group + i, 0, 0))
    n_lead = 2 + 2 + len(pieces) + 2
    return pl.pallas_call(
        functools.partial(interleave_kernel, chunk, len(bufs)),
        out_shape=[jax.ShapeDtypeStruct((batch, seq_part * heads, head_dim), jnp.bfloat16)] * 2,
        grid_spec=pltpu.PrefetchScalarGridSpec(
            num_scalar_prefetch=2,
            grid=(size // group,),
            in_specs=[own] * 2 + [piece] * len(pieces) + [whole] * 2 + [ANY] * len(bufs),
            out_specs=[out] * 2,
            scratch_shapes=[pltpu.VMEM((seq_part * heads, head_dim), jnp.float32), pltpu.VMEM((batch, head_dim), jnp.float32)],
        ),
        input_output_aliases={n_lead + i: i for i in range(len(bufs))},
        cost_estimate=pl.CostEstimate(flops=10**6 * size, bytes_accessed=16 * size * seq_part * head_dim * 2, transcendentals=0),
    )(me, lens, k_cache, v_cache, *pieces, k_new, v_new, *bufs)


def last_kernel(req, row0, *refs):
    count = len(PEERS) + 1
    pieces, outs, (mixed, staged, sems) = refs[:count], refs[count + 2 : count + 4], refs[count + 4 :]
    me = lax.axis_index("tp")
    rows = pieces[0].shape[2]
    copies = []
    for t in range(2):
        for piece, x in zip(pieces, PEERS + (0,)):
            mixed[t, pl.ds(me ^ x, rows, count), :] = piece[t, 0].astype(jnp.float32)
        staged[t] = mixed[t].astype(jnp.bfloat16)
        copies.append(pltpu.make_async_copy(staged.at[t], outs[t].at[req, pl.ds(row0 * count, rows * count)], sems.at[t]))
        copies[t].start()
    for copy in copies:
        copy.wait()


def interleave_last(pieces, bufs, row0):
    _, _, rows, head_dim = pieces[0].shape
    count = len(pieces)
    return pl.pallas_call(
        functools.partial(last_kernel, LAST[0], row0),
        out_shape=[jax.ShapeDtypeStruct(b.shape, b.dtype) for b in bufs],
        in_specs=[pl.BlockSpec(memory_space=pltpu.VMEM)] * count + [ANY] * 2,
        out_specs=[ANY] * 2,
        scratch_shapes=[
            pltpu.VMEM((2, rows * count, head_dim), jnp.float32),
            pltpu.VMEM((2, rows * count, head_dim), jnp.bfloat16),
            pltpu.SemaphoreType.DMA((2,)),
        ],
        input_output_aliases={count + i: i for i in range(2)},
        cost_estimate=pl.CostEstimate(flops=10**6, bytes_accessed=16 * rows * head_dim * 2, transcendentals=0),
    )(*(pltpu.with_memory_space_constraint(p, pltpu.VMEM) for p in pieces), *bufs)


def solution(mesh):
    n_tp = mesh.shape["tp"]

    def local_step(query, k_cache, v_cache, k_new, v_new, lens):
        batch, seq_len, _, head_dim = k_cache.shape
        seq_part = seq_len // n_tp
        heads = query.shape[1]
        me = lax.axis_index("tp").astype(jnp.int32).reshape(1)
        k_cache, v_cache = k_cache.reshape(batch, seq_len, head_dim), v_cache.reshape(batch, seq_len, head_dim)
        k_new, v_new = k_new.reshape(batch, head_dim), v_new.reshape(batch, head_dim)
        rows = jnp.pad(query, ((0, 0), (0, 8 - heads), (0, 0)))

        def send(pieces, peers=PEERS):
            moved = []
            for piece, x in zip(pieces, peers):
                moved.append(lax.ppermute(piece, "tp", [(i, i ^ x) for i in range(n_tp)]))
            return moved

        operands = lens, rows, k_cache, v_cache, k_new, v_new
        full = ((0, seq_part),)
        arrived, out = [[]], ()
        for peers in FIRST_PEERS:
            pieces = first_pieces(lens, k_cache, v_cache, k_new, v_new, FIRST, peers, pltpu.VMEM, seq_part)
            arrived[0] += send(pieces, peers)
        for n, chunk in enumerate(CHUNKS, 1):
            if n == 1:
                pieces = first_pieces(lens, k_cache, v_cache, k_new, v_new, chunk, PEERS, jax.ShapeDtypeStruct, seq_part)
            else:
                results = attend(*operands, chunk, full, seq_part, buf=out, sent=CHUNKS[0][1] if n == 2 else 0)
                out, pieces = results[:1], results[1:]
            arrived.append(send(pieces))

        unit = seq_part // sum(LAST_SPLIT)
        ranges = [(sum(LAST_SPLIT[:i]) * unit, share * unit) for i, share in enumerate(LAST_SPLIT)]
        count = len(PEERS) + 1
        out, *pieces = attend(*operands, LAST, ranges, seq_part, 1, out, (arrived[LAST_AFTER][0],))
        last_pieces = []
        for i in range(len(ranges)):
            mine = pieces[i * count : (i + 1) * count]
            last_pieces.append(send(mine[:-1]) + mine[-1:])

        bufs = ()
        for chunk, pieces in zip((FIRST, *CHUNKS), arrived):
            bufs = interleave(me, lens, k_cache, v_cache, pieces, k_new, v_new, bufs, chunk, seq_part)
        for (row0, _), pieces in zip(ranges, last_pieces):
            bufs = interleave_last(pieces, bufs, row0)
        k_seq, v_seq = (b.reshape(batch, seq_part, n_tp, head_dim) for b in bufs)
        return out[:, :heads], k_seq, v_seq

    head_spec = P("dp", "tp")
    entry_spec = P("dp", None, "tp")
    return jax.shard_map(local_step, mesh=mesh, in_specs=(head_spec, entry_spec, entry_spec, head_spec, head_spec, P("dp")), out_specs=(head_spec, P("dp", "tp"), P("dp", "tp")), check_vma=False)
```

profile of v0, /device:TPU:0, one launch (start us, length us, event | category | flops | bytes accessed | tf_op | source)
XLA Modules:
  0.0 834.3 jit_solution(16685377817868409372)
XLA Ops:
  2.3 35.5 %shard_map.85 = (bf16[64,8,128]{2,1,0:T(8,128)(2,1)}, bf16[2,36,512,128]{3,2,1,0:T(8,128)(2,1)}, bf16[2,36,512,128]{3,2,1,0:T(8,128)(2,1)}, bf16[2,36,512,128]{3,2,1,0:T(8,128)(2,1)}) custom-call(s32[64]{0:T(128)} %lens_ref.17, bf16[64,8,128]{2,1,0:T(8,128)(2,1)} %pad.4.q_ref, bf16[64,2048,128]{2,1,0:T(8,128)(2,1)} %bitcast.8, ...), custom_call_target="tpu_custom_call" | custom-call | flops 40000000 | bytes 73400320 | tf_op jit(solution)/shard_map/pallas_call | solution.py:109
  37.8 3.3 collective-permute-start
  42.5 1.6 collective-permute-start.19
  44.6 20.0 %shard_map.86 = (bf16[64,8,128]{2,1,0:T(8,128)(2,1)}, bf16[2,20,512,128]{3,2,1,0:T(8,128)(2,1)}, bf16[2,20,512,128]{3,2,1,0:T(8,128)(2,1)}, bf16[2,20,512,128]{3,2,1,0:T(8,128)(2,1)}) custom-call(s32[64]{0:T(128)} %lens_ref.17, bf16[64,8,128]{2,1,0:T(8,128)(2,1)} %pad.4.q_ref, bf16[64,2048,128]{2,1,0:T(8,128)(2,1)} %bitcast.10, ...), custom_call_target="tpu_custom_call", output_to_operand_aliasing={{0}: (6, {})} | custom-call | flops 20000000 | bytes 36700160 | tf_op jit(solution)/shard_map/pallas_call | solution.py:109
  64.6 4.2 shard_map.87
  68.7 382.5 %collective-permute-done.19.refs_3_ = bf16[2,1,512,128]{3,2,1,0:T(8,128)(2,1)S(1)} collective-permute-done((bf16[2,1,512,128]{3,2,1,0:T(8,128)(2,1)S(1)}, bf16[2,1,512,128]{3,2,1,0:T(8,128)(2,1)S(1)}, u32[]{:S(2)}, u32[]{:S(2)}) %collective-permute-start.19) | collective-permute-done | bytes 262176 | tf_op jit(solution)/shard_map/ppermute | solution.py:223
  454.4 17.1 %collective-permute-done.18.refs_2_ = bf16[2,1,512,128]{3,2,1,0:T(8,128)(2,1)S(1)} collective-permute-done((bf16[2,1,512,128]{3,2,1,0:T(8,128)(2,1)S(1)}, bf16[2,1,512,128]{3,2,1,0:T(8,128)(2,1)S(1)}, u32[]{:S(2)}, u32[]{:S(2)}) %collective-permute-start.18) | collective-permute-done | bytes 262176 | tf_op jit(solution)/shard_map/ppermute | solution.py:223
  472.9 3.9 shard_map.89
  478.0 7.6 collective-permute-done.8.refs_3_
  485.7 1.7 collective-permute-done.9.refs_4_
  487.5 1.5 collective-permute-start.16
  489.0 19.4 %collective-permute-done.15.refs_2_ = bf16[2,4,512,128]{3,2,1,0:T(8,128)(2,1)S(1)} collective-permute-done((bf16[2,4,512,128]{3,2,1,0:T(8,128)(2,1)}, bf16[2,4,512,128]{3,2,1,0:T(8,128)(2,1)S(1)}, u32[]{:S(2)}, u32[]{:S(2)}) %collective-permute-start.15) | collective-permute-done | bytes 1048608 | tf_op jit(solution)/shard_map/ppermute | solution.py:223
  508.4 22.1 %collective-permute-done.16.refs_3_ = bf16[2,4,512,128]{3,2,1,0:T(8,128)(2,1)S(1)} collective-permute-done((bf16[2,4,512,128]{3,2,1,0:T(8,128)(2,1)}, bf16[2,4,512,128]{3,2,1,0:T(8,128)(2,1)S(1)}, u32[]{:S(2)}, u32[]{:S(2)}) %collective-permute-start.16) | collective-permute-done | bytes 1048608 | tf_op jit(solution)/shard_map/ppermute | solution.py:223
  533.0 4.1 shard_map.88
  537.1 109.6 %collective-permute-done.10.refs_2_ = bf16[2,20,512,128]{3,2,1,0:T(8,128)(2,1)} collective-permute-done((bf16[2,20,512,128]{3,2,1,0:T(8,128)(2,1)}, bf16[2,20,512,128]{3,2,1,0:T(8,128)(2,1)}, u32[]{:S(2)}, u32[]{:S(2)}) %collective-permute-start.10) | collective-permute-done | bytes 5242912 | tf_op jit(solution)/shard_map/ppermute | solution.py:223
  648.2 109.9 %collective-permute-done.11.refs_3_ = bf16[2,20,512,128]{3,2,1,0:T(8,128)(2,1)} collective-permute-done((bf16[2,20,512,128]{3,2,1,0:T(8,128)(2,1)}, bf16[2,20,512,128]{3,2,1,0:T(8,128)(2,1)}, u32[]{:S(2)}, u32[]{:S(2)}) %collective-permute-start.11) | collective-permute-done | bytes 5242912 | tf_op jit(solution)/shard_map/ppermute | solution.py:223
  758.1 1.9 collective-permute-start.5
  763.2 3.2 shard_map.92
  766.4 6.5 shard_map.93
  773.5 32.9 %shard_map.94 = (bf16[64,2048,128]{2,1,0:T(8,128)(2,1)}, bf16[64,2048,128]{2,1,0:T(8,128)(2,1)}) custom-call(s32[1]{0:T(128)} %bitcast.4.me_ref, s32[64]{0:T(128)} %lens_ref.17, bf16[64,2048,128]{2,1,0:T(8,128)(2,1)} %bitcast.17, bf16[64,2048,128]{2,1,0:T(8,128)(2,1)} %bitcast.29, ...), custom_call_target="tpu_custom_call", output_to_operand_aliasing={{0}: (9, {}), {1}: (10, {})} | custom-call | flops 36000000 | bytes 75497472 | tf_op jit(solution)/shard_map/pallas_call | solution.py:159
  806.4 19.6 %shard_map.95 = (bf16[64,2048,128]{2,1,0:T(8,128)(2,1)}, bf16[64,2048,128]{2,1,0:T(8,128)(2,1)}) custom-call(s32[1]{0:T(128)} %bitcast.4.me_ref, s32[64]{0:T(128)} %lens_ref.17, bf16[64,2048,128]{2,1,0:T(8,128)(2,1)} %bitcast.18, bf16[64,2048,128]{2,1,0:T(8,128)(2,1)} %bitcast.30, ...), custom_call_target="tpu_custom_call", output_to_operand_aliasing={{0}: (9, {}), {1}: (10, {})} | custom-call | flops 20000000 | bytes 41943040 | tf_op jit(solution)/shard_map/pallas_call | solution.py:159
  826.0 4.4 shard_map.96
  830.3 2.1 shard_map.97
  832.5 1.8 shard_map.98
  (63 shorter events, 17.2 us)
Async XLA Ops:
  37.8 494.2 %collective-permute-start = (bf16[2,36,512,128]{3,2,1,0:T(8,128)(2,1)}, bf16[2,36,512,128]{3,2,1,0:T(8,128)(2,1)}, u32[]{:S(2)}, u32[]{:S(2)}) collective-permute-start(bf16[2,36,512,128]{3,2,1,0:T(8,128)(2,1)} %get-tuple-element.46), channel_id=1, source_target_pairs={{0,2},{1,3},{2,0},{3,1},{4,6},{5,7},{6,4},{7,5}} | collective-permute-start | bytes 28311560 | tf_op jit(solution)/shard_map/ppermute | solution.py:223
  41.1 718.9 %collective-permute-start.13 = (bf16[2,36,512,128]{3,2,1,0:T(8,128)(2,1)}, bf16[2,36,512,128]{3,2,1,0:T(8,128)(2,1)}, u32[]{:S(2)}, u32[]{:S(2)}) collective-permute-start(bf16[2,36,512,128]{3,2,1,0:T(8,128)(2,1)} %get-tuple-element.62), channel_id=1, source_target_pairs={{0,3},{1,2},{2,1},{3,0},{4,7},{5,6},{6,5},{7,4}} | collective-permute-start | bytes 28311560 | tf_op jit(solution)/shard_map/ppermute | solution.py:223
  41.1 719.5 %collective-permute-start.14 = (bf16[2,36,512,128]{3,2,1,0:T(8,128)(2,1)}, bf16[2,36,512,128]{3,2,1,0:T(8,128)(2,1)}, u32[]{:S(2)}, u32[]{:S(2)}) collective-permute-start(bf16[2,36,512,128]{3,2,1,0:T(8,128)(2,1)} %get-tuple-element.63), channel_id=1, source_target_pairs={{0,1},{1,0},{2,3},{3,2},{4,5},{5,4},{6,7},{7,6}} | collective-permute-start | bytes 28311560 | tf_op jit(solution)/shard_map/ppermute | solution.py:223
  42.5 408.8 %collective-permute-start.19 = (bf16[2,1,512,128]{3,2,1,0:T(8,128)(2,1)S(1)}, bf16[2,1,512,128]{3,2,1,0:T(8,128)(2,1)S(1)}, u32[]{:S(2)}, u32[]{:S(2)}) collective-permute-start(bf16[2,1,512,128]{3,2,1,0:T(8,128)(2,1)S(1)} %get-tuple-element.67), channel_id=1, source_target_pairs={{0,3},{1,2},{2,1},{3,0},{4,7},{5,6},{6,5},{7,4}} | collective-permute-start | bytes 786440 | tf_op jit(solution)/shard_map/ppermute | solution.py:223
  44.1 409.6 %collective-permute-start.20 = (bf16[2,1,512,128]{3,2,1,0:T(8,128)(2,1)S(1)}, bf16[2,1,512,128]{3,2,1,0:T(8,128)(2,1)S(1)}, u32[]{:S(2)}, u32[]{:S(2)}) collective-permute-start(bf16[2,1,512,128]{3,2,1,0:T(8,128)(2,1)S(1)} %get-tuple-element.68), channel_id=1, source_target_pairs={{0,1},{1,0},{2,3},{3,2},{4,5},{5,4},{6,7},{7,6}} | collective-permute-start | bytes 786440 | tf_op jit(solution)/shard_map/ppermute | solution.py:223
  451.3 25.5 %collective-permute-start.7 = (bf16[2,2,512,128]{3,2,1,0:T(8,128)(2,1)}, bf16[2,2,512,128]{3,2,1,0:T(8,128)(2,1)S(1)}, u32[]{:S(2)}, u32[]{:S(2)}) collective-permute-start(bf16[2,2,512,128]{3,2,1,0:T(8,128)(2,1)} %get-tuple-element.56), channel_id=1, source_target_pairs={{0,2},{1,3},{2,0},{3,1},{4,6},{5,7},{6,4},{7,5}} | collective-permute-start | bytes 1572872 | tf_op jit(solution)/shard_map/ppermute | solution.py:223
  453.6 23.1 %copy-start.10 = (bf16[2,1,512,128]{3,2,1,0:T(8,128)(2,1)}, bf16[2,1,512,128]{3,2,1,0:T(8,128)(2,1)S(1)}, u32[]{:S(2)}) copy-start(bf16[2,1,512,128]{3,2,1,0:T(8,128)(2,1)S(1)} %collective-permute-done.20.refs_4_) | copy-start | bytes 786436
  453.6 17.9 %collective-permute-start.18 = (bf16[2,1,512,128]{3,2,1,0:T(8,128)(2,1)S(1)}, bf16[2,1,512,128]{3,2,1,0:T(8,128)(2,1)S(1)}, u32[]{:S(2)}, u32[]{:S(2)}) collective-permute-start(bf16[2,1,512,128]{3,2,1,0:T(8,128)(2,1)S(1)} %shard_map.90), channel_id=1, source_target_pairs={{0,2},{1,3},{2,0},{3,1},{4,6},{5,7},{6,4},{7,5}} | collective-permute-start | bytes 786440 | tf_op jit(solution)/shard_map/ppermute | solution.py:223
  471.5 14.0 %collective-permute-start.8 = (bf16[2,2,512,128]{3,2,1,0:T(8,128)(2,1)S(1)}, bf16[2,2,512,128]{3,2,1,0:T(8,128)(2,1)S(1)}, u32[]{:S(2)}, u32[]{:S(2)}) collective-permute-start(bf16[2,2,512,128]{3,2,1,0:T(8,128)(2,1)S(1)} %copy-done.13), channel_id=1, source_target_pairs={{0,3},{1,2},{2,1},{3,0},{4,7},{5,6},{6,5},{7,4}} | collective-permute-start | bytes 1572872 | tf_op jit(solution)/shard_map/ppermute | solution.py:223
  477.6 30.8 %collective-permute-start.15 = (bf16[2,4,512,128]{3,2,1,0:T(8,128)(2,1)}, bf16[2,4,512,128]{3,2,1,0:T(8,128)(2,1)S(1)}, u32[]{:S(2)}, u32[]{:S(2)}) collective-permute-start(bf16[2,4,512,128]{3,2,1,0:T(8,128)(2,1)} %get-tuple-element.64), channel_id=1, source_target_pairs={{0,2},{1,3},{2,0},{3,1},{4,6},{5,7},{6,4},{7,5}} | collective-permute-start | bytes 3145736 | tf_op jit(solution)/shard_map/ppermute | solution.py:223
  485.6 47.1 %copy-start.7 = (bf16[2,2,512,128]{3,2,1,0:T(8,128)(2,1)}, bf16[2,2,512,128]{3,2,1,0:T(8,128)(2,1)S(1)}, u32[]{:S(2)}) copy-start(bf16[2,2,512,128]{3,2,1,0:T(8,128)(2,1)S(1)} %collective-permute-done.8.refs_3_) | copy-start | bytes 1572868
  485.6 1.9 collective-permute-start.9
  487.5 43.0 %collective-permute-start.16 = (bf16[2,4,512,128]{3,2,1,0:T(8,128)(2,1)}, bf16[2,4,512,128]{3,2,1,0:T(8,128)(2,1)S(1)}, u32[]{:S(2)}, u32[]{:S(2)}) collective-permute-start(bf16[2,4,512,128]{3,2,1,0:T(8,128)(2,1)} %get-tuple-element.65), channel_id=1, source_target_pairs={{0,3},{1,2},{2,1},{3,0},{4,7},{5,6},{6,5},{7,4}} | collective-permute-start | bytes 3145736 | tf_op jit(solution)/shard_map/ppermute | solution.py:223
  508.4 28.7 %copy-start.3 = (bf16[2,4,512,128]{3,2,1,0:T(8,128)(2,1)}, bf16[2,4,512,128]{3,2,1,0:T(8,128)(2,1)S(1)}, u32[]{:S(2)}) copy-start(bf16[2,4,512,128]{3,2,1,0:T(8,128)(2,1)S(1)} %collective-permute-done.15.refs_2_) | copy-start | bytes 3145732
  508.4 23.6 %collective-permute-start.17 = (bf16[2,4,512,128]{3,2,1,0:T(8,128)(2,1)}, bf16[2,4,512,128]{3,2,1,0:T(8,128)(2,1)S(1)}, u32[]{:S(2)}, u32[]{:S(2)}) collective-permute-start(bf16[2,4,512,128]{3,2,1,0:T(8,128)(2,1)} %get-tuple-element.66), channel_id=1, source_target_pairs={{0,1},{1,0},{2,3},{3,2},{4,5},{5,4},{6,7},{7,6}} | collective-permute-start | bytes 3145736 | tf_op jit(solution)/shard_map/ppermute | solution.py:223
  530.5 116.2 %collective-permute-start.10 = (bf16[2,20,512,128]{3,2,1,0:T(8,128)(2,1)}, bf16[2,20,512,128]{3,2,1,0:T(8,128)(2,1)}, u32[]{:S(2)}, u32[]{:S(2)}) collective-permute-start(bf16[2,20,512,128]{3,2,1,0:T(8,128)(2,1)} %get-tuple-element.59), channel_id=1, source_target_pairs={{0,2},{1,3},{2,0},{3,1},{4,6},{5,7},{6,4},{7,5}} | collective-permute-start | bytes 15728648 | tf_op jit(solution)/shard_map/ppermute | solution.py:223
  532.0 226.1 %collective-permute-start.11 = (bf16[2,20,512,128]{3,2,1,0:T(8,128)(2,1)}, bf16[2,20,512,128]{3,2,1,0:T(8,128)(2,1)}, u32[]{:S(2)}, u32[]{:S(2)}) collective-permute-start(bf16[2,20,512,128]{3,2,1,0:T(8,128)(2,1)} %get-tuple-element.60), channel_id=1, source_target_pairs={{0,3},{1,2},{2,1},{3,0},{4,7},{5,6},{6,5},{7,4}} | collective-permute-start | bytes 15728648 | tf_op jit(solution)/shard_map/ppermute | solution.py:223
  532.0 228.0 %collective-permute-start.12 = (bf16[2,20,512,128]{3,2,1,0:T(8,128)(2,1)}, bf16[2,20,512,128]{3,2,1,0:T(8,128)(2,1)}, u32[]{:S(2)}, u32[]{:S(2)}) collective-permute-start(bf16[2,20,512,128]{3,2,1,0:T(8,128)(2,1)} %get-tuple-element.61), channel_id=1, source_target_pairs={{0,1},{1,0},{2,3},{3,2},{4,5},{5,4},{6,7},{7,6}} | collective-permute-start | bytes 15728648 | tf_op jit(solution)/shard_map/ppermute | solution.py:223
  646.7 115.8 %collective-permute-start.4 = (bf16[2,1,352,128]{3,2,1,0:T(8,128)(2,1)}, bf16[2,1,352,128]{3,2,1,0:T(8,128)(2,1)S(1)}, u32[]{:S(2)}, u32[]{:S(2)}) collective-permute-start(bf16[2,1,352,128]{3,2,1,0:T(8,128)(2,1)} %get-tuple-element.52), channel_id=1, source_target_pairs={{0,2},{1,3},{2,0},{3,1},{4,6},{5,7},{6,4},{7,5}} | collective-permute-start | bytes 540680 | tf_op jit(solution)/shard_map/ppermute | solution.py:223
  758.1 72.2 %collective-permute-start.5 = (bf16[2,1,352,128]{3,2,1,0:T(8,128)(2,1)}, bf16[2,1,352,128]{3,2,1,0:T(8,128)(2,1)}, u32[]{:S(2)}, u32[]{:S(2)}) collective-permute-start(bf16[2,1,352,128]{3,2,1,0:T(8,128)(2,1)} %get-tuple-element.53), channel_id=1, source_target_pairs={{0,3},{1,2},{2,1},{3,0},{4,7},{5,6},{6,5},{7,4}} | collective-permute-start | bytes 540680 | tf_op jit(solution)/shard_map/ppermute | solution.py:223
  760.0 70.3 %collective-permute-start.6 = (bf16[2,1,352,128]{3,2,1,0:T(8,128)(2,1)}, bf16[2,1,352,128]{3,2,1,0:T(8,128)(2,1)}, u32[]{:S(2)}, u32[]{:S(2)}) collective-permute-start(bf16[2,1,352,128]{3,2,1,0:T(8,128)(2,1)} %get-tuple-element.54), channel_id=1, source_target_pairs={{0,1},{1,0},{2,3},{3,2},{4,5},{5,4},{6,7},{7,6}} | collective-permute-start | bytes 540680 | tf_op jit(solution)/shard_map/ppermute | solution.py:223
  760.0 72.4 %collective-permute-start.1 = (bf16[2,1,160,128]{3,2,1,0:T(8,128)(2,1)}, bf16[2,1,160,128]{3,2,1,0:T(8,128)(2,1)}, u32[]{:S(2)}, u32[]{:S(2)}) collective-permute-start(bf16[2,1,160,128]{3,2,1,0:T(8,128)(2,1)} %get-tuple-element.48), channel_id=1, source_target_pairs={{0,2},{1,3},{2,0},{3,1},{4,6},{5,7},{6,4},{7,5}} | collective-permute-start | bytes 245768 | tf_op jit(solution)/shard_map/ppermute | solution.py:223
  760.6 71.9 %collective-permute-start.2 = (bf16[2,1,160,128]{3,2,1,0:T(8,128)(2,1)}, bf16[2,1,160,128]{3,2,1,0:T(8,128)(2,1)}, u32[]{:S(2)}, u32[]{:S(2)}) collective-permute-start(bf16[2,1,160,128]{3,2,1,0:T(8,128)(2,1)} %get-tuple-element.49), channel_id=1, source_target_pairs={{0,3},{1,2},{2,1},{3,0},{4,7},{5,6},{6,5},{7,4}} | collective-permute-start | bytes 245768 | tf_op jit(solution)/shard_map/ppermute | solution.py:223
  763.2 69.3 %collective-permute-start.3 = (bf16[2,1,160,128]{3,2,1,0:T(8,128)(2,1)}, bf16[2,1,160,128]{3,2,1,0:T(8,128)(2,1)}, u32[]{:S(2)}, u32[]{:S(2)}) collective-permute-start(bf16[2,1,160,128]{3,2,1,0:T(8,128)(2,1)} %get-tuple-element.50), channel_id=1, source_target_pairs={{0,1},{1,0},{2,3},{3,2},{4,5},{5,4},{6,7},{7,6}} | collective-permute-start | bytes 245768 | tf_op jit(solution)/shard_map/ppermute | solution.py:223
  (11 other events, 82.6 us)
where the time goes:
time: 835 us; the launch traced here: 834 us
  waiting for transfers between devices  671 us (80%)
  Pallas kernels  140 us (17%)
  starting transfers between devices  18.4 us (2%)
    ppermute x21, waiting for transfers between devices, send(): moved.append(lax.ppermute(piece, 'tp', [(i, i ^ x) for i in range(n_tp)]))  671 us
    pallas_call x5, Pallas kernels, interleave(): pl.pallas_call(functools.partial(interleave_kernel, chunk, len(bufs)), ou...  66.5 us
    pallas_call x4, Pallas kernels, attend(): pl.pallas_call(functools.partial(attend_kernel, first, group, seq_part, [...  63.7 us
    ppermute x21, starting transfers between devices, send(): moved.append(lax.ppermute(piece, 'tp', [(i, i ^ x) for i in range(n_tp)]))  18.4 us
  transfers between devices with their start and end apart: 21, of which 9 were waited for; matrix products, arithmetic and copies ran while one was open for 0% of the time, Pallas kernels for 12%

commit v1 on v0

--- a/solution.py
+++ b/solution.py
@@ -10,7 +10,8 @@
 
 FIRST = (63, 1, 1)
 CHUNKS = ((0, 4, 4), (4, 36, 4), (40, 20, 4), (60, 2, 2))
-LAST = (62, 2, 2)
+LAST = (62, 1, 1)
+TAIL = (60, 4, 4)
 LAST_SPLIT = (11, 5)
 LAST_AFTER = 2
 PEERS = (2, 3, 1)
@@ -29,16 +30,16 @@
         ref[window] = jnp.where(at, row, old).astype(ref.dtype)
 
 
-def first_kernel(req, size, seq_part, peers, lens_hbm, k_hbm, v_hbm, k_new_hbm, v_new_hbm, *refs):
-    outs, (lens, new_rows, sems) = refs[: len(peers)], refs[len(peers) :]
+def first_kernel(req, size, seq_part, parts, n_skip, lens_hbm, k_hbm, v_hbm, k_new_hbm, v_new_hbm, *refs):
+    outs, (lens, new_rows, sems) = refs[n_skip:-3], refs[-3:]
     me = lax.axis_index("tp")
     base = req // ROWS * ROWS
     copies = [pltpu.make_async_copy(lens_hbm, lens, sems.at[0])]
     for t, (cache, new) in enumerate(((k_hbm, k_new_hbm), (v_hbm, v_new_hbm))):
         copies.append(pltpu.make_async_copy(new.at[pl.ds(base, ROWS)], new_rows.at[t], sems.at[1 + t]))
-        for i, x in enumerate(peers):
-            piece = cache.at[pl.ds(req, size), pl.ds((me ^ x) * seq_part, seq_part)]
-            copies.append(pltpu.make_async_copy(piece, outs[i].at[t], sems.at[3 + t * len(peers) + i]))
+        for i, (x, row0, n) in enumerate(parts):
+            piece = cache.at[pl.ds(req, size), pl.ds((me ^ x) * seq_part + row0, n)]
+            copies.append(pltpu.make_async_copy(piece, outs[i].at[t], sems.at[3 + t * len(parts) + i]))
     for copy in copies:
         copy.start()
     for copy in copies:
@@ -46,21 +47,21 @@
     for t in range(2):
         for r in range(size):
             row = new_rows[t, pl.ds(req + r - base, 1), :].astype(jnp.float32)
-            for i, x in enumerate(peers):
-                put_row(outs[i], (t, r), lens[req + r] - (me ^ x) * seq_part, row)
-
-
-def first_pieces(lens, k_cache, v_cache, k_new, v_new, chunk, peers, make, seq_part):
+            for i, (x, row0, _) in enumerate(parts):
+                put_row(outs[i], (t, r), lens[req + r] - (me ^ x) * seq_part - row0, row)
+
+
+def first_pieces(lens, k_cache, v_cache, k_new, v_new, chunk, parts, in_vmem, seq_part, after=()):
     first, size, _ = chunk
     head_dim = k_new.shape[-1]
-    count = len(peers)
-    return pl.pallas_call(
-        functools.partial(first_kernel, first, size, seq_part, peers),
-        out_shape=[make((2, size, seq_part, head_dim), jnp.bfloat16)] * count,
-        in_specs=[ANY] * 5,
+    count = len(parts)
+    return pl.pallas_call(
+        functools.partial(first_kernel, first, size, seq_part, parts, len(after)),
+        out_shape=[(pltpu.VMEM if in_vmem or not x else jax.ShapeDtypeStruct)((2, size, n, head_dim), jnp.bfloat16) for x, _, n in parts],
+        in_specs=[ANY] * (5 + len(after)),
         out_specs=[pl.BlockSpec(memory_space=pltpu.VMEM)] * count,
         scratch_shapes=[pltpu.SMEM(lens.shape, jnp.int32), pltpu.VMEM((2, ROWS, head_dim), jnp.bfloat16), pltpu.SemaphoreType.DMA((3 + 2 * count,))],
-    )(lens, k_cache, v_cache, k_new, v_new)
+    )(lens, k_cache, v_cache, k_new, v_new, *after)
 
 
 def attend_kernel(first, group, seq_part, parts, n_skip, lens_ref, q_ref, k_ref, v_ref, k_new_ref, v_new_ref, *refs):
@@ -95,17 +96,17 @@
         out_ref[r] = out.astype(jnp.bfloat16)
 
 
-def attend(lens, query, k_cache, v_cache, k_new, v_new, chunk, ranges, seq_part, n_own=0, buf=(), after=(), sent=0):
+def attend(lens, query, k_cache, v_cache, k_new, v_new, chunk, ranges, seq_part, n_sent=0, buf=(), after=(), sent=0):
     first, size, group = chunk[0] - sent, chunk[1] + sent, chunk[2]
     batch, seq_len, head_dim = k_cache.shape
     rows = query.shape[1]
-    parts = [(x, row0, n) for row0, n in ranges for x in PEERS + (0,) * (n_own > 0)]
+    parts = [(x, row0, n) for row0, n in ranges for x in PEERS]
     at = lambda i, lens: (first // group + i, 0, 0)
     cache = pl.BlockSpec((group, seq_len, head_dim), at)
     heads = pl.BlockSpec((group, rows, head_dim), at)
     whole = pl.BlockSpec((batch, head_dim), lambda i, lens: (0, 0))
-    piece = lambda x, n: pl.BlockSpec((2, n_own or group, n, head_dim), lambda i, lens: (0, jnp.maximum(i - sent // group, 0), 0, 0)) if x else pl.BlockSpec(memory_space=pltpu.VMEM)
-    shape = lambda x, n: (jax.ShapeDtypeStruct if x else pltpu.VMEM)((2, n_own or size - sent, n, head_dim), jnp.bfloat16)
+    piece = lambda x, n: pl.BlockSpec((2, n_sent or group, n, head_dim), lambda i, lens: (0, jnp.maximum(i - sent // group, 0), 0, 0)) if x else pl.BlockSpec(memory_space=pltpu.VMEM)
+    shape = lambda x, n: (jax.ShapeDtypeStruct if x else pltpu.VMEM)((2, n_sent or size - sent, n, head_dim), jnp.bfloat16)
     return pl.pallas_call(
         functools.partial(attend_kernel, first, group, seq_part, [p[:2] for p in parts], len(buf) + len(after)),
         out_shape=[jax.ShapeDtypeStruct(query.shape, jnp.bfloat16)] + [shape(x, n) for x, _, n in parts],
@@ -227,20 +228,21 @@
         full = ((0, seq_part),)
         arrived, out = [[]], ()
         for peers in FIRST_PEERS:
-            pieces = first_pieces(lens, k_cache, v_cache, k_new, v_new, FIRST, peers, pltpu.VMEM, seq_part)
+            pieces = first_pieces(lens, k_cache, v_cache, k_new, v_new, FIRST, [(x, 0, seq_part) for x in peers], True, seq_part)
             arrived[0] += send(pieces, peers)
         for n, chunk in enumerate(CHUNKS, 1):
             if n == 1:
-                pieces = first_pieces(lens, k_cache, v_cache, k_new, v_new, chunk, PEERS, jax.ShapeDtypeStruct, seq_part)
+                pieces = first_pieces(lens, k_cache, v_cache, k_new, v_new, chunk, [(x, 0, seq_part) for x in PEERS], False, seq_part)
             else:
-                results = attend(*operands, chunk, full, seq_part, buf=out, sent=CHUNKS[0][1] if n == 2 else 0)
+                results = attend(*operands, TAIL if n == len(CHUNKS) else chunk, full, seq_part, chunk[1] if n == len(CHUNKS) else 0, out, (), CHUNKS[0][1] if n == 2 else 0)
                 out, pieces = results[:1], results[1:]
             arrived.append(send(pieces))
 
         unit = seq_part // sum(LAST_SPLIT)
         ranges = [(sum(LAST_SPLIT[:i]) * unit, share * unit) for i, share in enumerate(LAST_SPLIT)]
         count = len(PEERS) + 1
-        out, *pieces = attend(*operands, LAST, ranges, seq_part, 1, out, (arrived[LAST_AFTER][0],))
+        parts = [(x, row0, share) for row0, share in ranges for x in PEERS + (0,)]
+        pieces = list(first_pieces(lens, k_cache, v_cache, k_new, v_new, LAST, parts, False, seq_part, (arrived[LAST_AFTER][0],)))
         last_pieces = []
         for i in range(len(ranges)):
             mine = pieces[i * count : (i + 1) * count]
@@ -252,7 +254,7 @@
         for (row0, _), pieces in zip(ranges, last_pieces):
             bufs = interleave_last(pieces, bufs, row0)
         k_seq, v_seq = (b.reshape(batch, seq_part, n_tp, head_dim) for b in bufs)
-        return out[:, :heads], k_seq, v_seq
+        return out[0][:, :heads], k_seq, v_seq
 
     head_spec = P("dp", "tp")
     entry_spec = P("dp", None, "tp")

time: 835 us -> 835 us (level)
    pallas_call x4 -> x3, Pallas kernels: 63.7 us -> 61.4 us  [attend(): pl.pallas_call(functools.partial(attend_kernel, first, group, seq_part, [...]
where the time goes in v1:
time: 835 us; the launch traced here: 834 us
  waiting for transfers between devices  670 us (80%)
  Pallas kernels  140 us (17%)
  starting transfers between devices  17.8 us (2%)
    ppermute x21, waiting for transfers between devices, send(): moved.append(lax.ppermute(piece, 'tp', [(i, i ^ x) for i in range(n_tp)]))  670 us
    pallas_call x5, Pallas kernels, interleave(): pl.pallas_call(functools.partial(interleave_kernel, chunk, len(bufs)), ou...  66.3 us
    pallas_call x3, Pallas kernels, attend(): pl.pallas_call(functools.partial(attend_kernel, first, group, seq_part, [...  61.4 us
    ppermute x21, starting transfers between devices, send(): moved.append(lax.ppermute(piece, 'tp', [(i, i ^ x) for i in range(n_tp)]))  17.8 us
  transfers between devices with their start and end apart: 21, of which 9 were waited for; matrix products, arithmetic and copies ran while one was open for 0% of the time, Pallas kernels for 12%

profile of v1, /device:TPU:0, one launch (start us, length us, event | category | flops | bytes accessed | tf_op | source)
XLA Modules:
  0.0 834.1 jit_solution(1601269083199329524)
XLA Ops:
  2.3 35.5 %shard_map.85 = (bf16[64,8,128]{2,1,0:T(8,128)(2,1)}, bf16[2,36,512,128]{3,2,1,0:T(8,128)(2,1)}, bf16[2,36,512,128]{3,2,1,0:T(8,128)(2,1)}, bf16[2,36,512,128]{3,2,1,0:T(8,128)(2,1)}) custom-call(s32[64]{0:T(128)} %lens_ref.15, bf16[64,8,128]{2,1,0:T(8,128)(2,1)} %pad.4.q_ref, bf16[64,2048,128]{2,1,0:T(8,128)(2,1)} %bitcast.8, ...), custom_call_target="tpu_custom_call" | custom-call | flops 40000000 | bytes 73400320 | tf_op jit(solution)/shard_map/pallas_call | solution.py:110
  37.8 3.3 collective-permute-start
  42.4 1.6 collective-permute-start.19
  44.6 20.0 %shard_map.86 = (bf16[64,8,128]{2,1,0:T(8,128)(2,1)}, bf16[2,20,512,128]{3,2,1,0:T(8,128)(2,1)}, bf16[2,20,512,128]{3,2,1,0:T(8,128)(2,1)}, bf16[2,20,512,128]{3,2,1,0:T(8,128)(2,1)}) custom-call(s32[64]{0:T(128)} %lens_ref.15, bf16[64,8,128]{2,1,0:T(8,128)(2,1)} %pad.4.q_ref, bf16[64,2048,128]{2,1,0:T(8,128)(2,1)} %bitcast.10, ...), custom_call_target="tpu_custom_call", output_to_operand_aliasing={{0}: (6, {})} | custom-call | flops 20000000 | bytes 36700160 | tf_op jit(solution)/shard_map/pallas_call | solution.py:110
  64.5 5.9 shard_map.87
  70.4 380.9 %collective-permute-done.19.refs_3_ = bf16[2,1,512,128]{3,2,1,0:T(8,128)(2,1)S(1)} collective-permute-done((bf16[2,1,512,128]{3,2,1,0:T(8,128)(2,1)S(1)}, bf16[2,1,512,128]{3,2,1,0:T(8,128)(2,1)S(1)}, u32[]{:S(2)}, u32[]{:S(2)}) %collective-permute-start.19) | collective-permute-done | bytes 262176 | tf_op jit(solution)/shard_map/ppermute | solution.py:224
  454.4 17.1 %collective-permute-done.18.refs_2_ = bf16[2,1,512,128]{3,2,1,0:T(8,128)(2,1)S(1)} collective-permute-done((bf16[2,1,512,128]{3,2,1,0:T(8,128)(2,1)S(1)}, bf16[2,1,512,128]{3,2,1,0:T(8,128)(2,1)S(1)}, u32[]{:S(2)}, u32[]{:S(2)}) %collective-permute-start.18) | collective-permute-done | bytes 262176 | tf_op jit(solution)/shard_map/ppermute | solution.py:224
  472.8 3.9 shard_map.89
  477.9 7.6 collective-permute-done.8.refs_3_
  485.7 1.7 collective-permute-done.9.refs_4_
  487.4 1.5 collective-permute-start.16
  489.0 19.4 %collective-permute-done.15.refs_2_ = bf16[2,4,512,128]{3,2,1,0:T(8,128)(2,1)S(1)} collective-permute-done((bf16[2,4,512,128]{3,2,1,0:T(8,128)(2,1)}, bf16[2,4,512,128]{3,2,1,0:T(8,128)(2,1)S(1)}, u32[]{:S(2)}, u32[]{:S(2)}) %collective-permute-start.15) | collective-permute-done | bytes 1048608 | tf_op jit(solution)/shard_map/ppermute | solution.py:224
  508.4 22.1 %collective-permute-done.16.refs_3_ = bf16[2,4,512,128]{3,2,1,0:T(8,128)(2,1)S(1)} collective-permute-done((bf16[2,4,512,128]{3,2,1,0:T(8,128)(2,1)}, bf16[2,4,512,128]{3,2,1,0:T(8,128)(2,1)S(1)}, u32[]{:S(2)}, u32[]{:S(2)}) %collective-permute-start.16) | collective-permute-done | bytes 1048608 | tf_op jit(solution)/shard_map/ppermute | solution.py:224
  533.0 2.5 shard_map.88
  535.5 111.2 %collective-permute-done.10.refs_2_ = bf16[2,20,512,128]{3,2,1,0:T(8,128)(2,1)} collective-permute-done((bf16[2,20,512,128]{3,2,1,0:T(8,128)(2,1)}, bf16[2,20,512,128]{3,2,1,0:T(8,128)(2,1)}, u32[]{:S(2)}, u32[]{:S(2)}) %collective-permute-start.10) | collective-permute-done | bytes 5242912 | tf_op jit(solution)/shard_map/ppermute | solution.py:224
  648.2 109.9 %collective-permute-done.11.refs_3_ = bf16[2,20,512,128]{3,2,1,0:T(8,128)(2,1)} collective-permute-done((bf16[2,20,512,128]{3,2,1,0:T(8,128)(2,1)}, bf16[2,20,512,128]{3,2,1,0:T(8,128)(2,1)}, u32[]{:S(2)}, u32[]{:S(2)}) %collective-permute-start.11) | collective-permute-done | bytes 5242912 | tf_op jit(solution)/shard_map/ppermute | solution.py:224
  758.1 1.9 collective-permute-start.5
  763.8 3.2 shard_map.92
  767.0 6.3 shard_map.93
  773.3 32.9 %shard_map.94 = (bf16[64,2048,128]{2,1,0:T(8,128)(2,1)}, bf16[64,2048,128]{2,1,0:T(8,128)(2,1)}) custom-call(s32[1]{0:T(128)} %bitcast.4.me_ref, s32[64]{0:T(128)} %lens_ref.15, bf16[64,2048,128]{2,1,0:T(8,128)(2,1)} %bitcast.17, bf16[64,2048,128]{2,1,0:T(8,128)(2,1)} %bitcast.29, ...), custom_call_target="tpu_custom_call", output_to_operand_aliasing={{0}: (9, {}), {1}: (10, {})} | custom-call | flops 36000000 | bytes 75497472 | tf_op jit(solution)/shard_map/pallas_call | solution.py:160
  806.2 19.6 %shard_map.95 = (bf16[64,2048,128]{2,1,0:T(8,128)(2,1)}, bf16[64,2048,128]{2,1,0:T(8,128)(2,1)}) custom-call(s32[1]{0:T(128)} %bitcast.4.me_ref, s32[64]{0:T(128)} %lens_ref.15, bf16[64,2048,128]{2,1,0:T(8,128)(2,1)} %bitcast.18, bf16[64,2048,128]{2,1,0:T(8,128)(2,1)} %bitcast.30, ...), custom_call_target="tpu_custom_call", output_to_operand_aliasing={{0}: (9, {}), {1}: (10, {})} | custom-call | flops 20000000 | bytes 41943040 | tf_op jit(solution)/shard_map/pallas_call | solution.py:160
  825.8 4.4 shard_map.96
  830.1 2.1 shard_map.97
  832.3 1.8 shard_map.98
  (63 shorter events, 17.2 us)
Async XLA Ops:
  37.8 494.2 %collective-permute-start = (bf16[2,36,512,128]{3,2,1,0:T(8,128)(2,1)}, bf16[2,36,512,128]{3,2,1,0:T(8,128)(2,1)}, u32[]{:S(2)}, u32[]{:S(2)}) collective-permute-start(bf16[2,36,512,128]{3,2,1,0:T(8,128)(2,1)} %get-tuple-element.45), channel_id=1, source_target_pairs={{0,2},{1,3},{2,0},{3,1},{4,6},{5,7},{6,4},{7,5}} | collective-permute-start | bytes 28311560 | tf_op jit(solution)/shard_map/ppermute | solution.py:224
  41.1 718.9 %collective-permute-start.13 = (bf16[2,36,512,128]{3,2,1,0:T(8,128)(2,1)}, bf16[2,36,512,128]{3,2,1,0:T(8,128)(2,1)}, u32[]{:S(2)}, u32[]{:S(2)}) collective-permute-start(bf16[2,36,512,128]{3,2,1,0:T(8,128)(2,1)} %get-tuple-element.60), channel_id=1, source_target_pairs={{0,3},{1,2},{2,1},{3,0},{4,7},{5,6},{6,5},{7,4}} | collective-permute-start | bytes 28311560 | tf_op jit(solution)/shard_map/ppermute | solution.py:224
  41.1 719.5 %collective-permute-start.14 = (bf16[2,36,512,128]{3,2,1,0:T(8,128)(2,1)}, bf16[2,36,512,128]{3,2,1,0:T(8,128)(2,1)}, u32[]{:S(2)}, u32[]{:S(2)}) collective-permute-start(bf16[2,36,512,128]{3,2,1,0:T(8,128)(2,1)} %get-tuple-element.61), channel_id=1, source_target_pairs={{0,1},{1,0},{2,3},{3,2},{4,5},{5,4},{6,7},{7,6}} | collective-permute-start | bytes 28311560 | tf_op jit(solution)/shard_map/ppermute | solution.py:224
  42.4 408.8 %collective-permute-start.19 = (bf16[2,1,512,128]{3,2,1,0:T(8,128)(2,1)S(1)}, bf16[2,1,512,128]{3,2,1,0:T(8,128)(2,1)S(1)}, u32[]{:S(2)}, u32[]{:S(2)}) collective-permute-start(bf16[2,1,512,128]{3,2,1,0:T(8,128)(2,1)S(1)} %get-tuple-element.65), channel_id=1, source_target_pairs={{0,3},{1,2},{2,1},{3,0},{4,7},{5,6},{6,5},{7,4}} | collective-permute-start | bytes 786440 | tf_op jit(solution)/shard_map/ppermute | solution.py:224
  44.0 409.6 %collective-permute-start.20 = (bf16[2,1,512,128]{3,2,1,0:T(8,128)(2,1)S(1)}, bf16[2,1,512,128]{3,2,1,0:T(8,128)(2,1)S(1)}, u32[]{:S(2)}, u32[]{:S(2)}) collective-permute-start(bf16[2,1,512,128]{3,2,1,0:T(8,128)(2,1)S(1)} %get-tuple-element.66), channel_id=1, source_target_pairs={{0,1},{1,0},{2,3},{3,2},{4,5},{5,4},{6,7},{7,6}} | collective-permute-start | bytes 786440 | tf_op jit(solution)/shard_map/ppermute | solution.py:224
  451.2 25.5 %collective-permute-start.7 = (bf16[2,2,512,128]{3,2,1,0:T(8,128)(2,1)}, bf16[2,2,512,128]{3,2,1,0:T(8,128)(2,1)S(1)}, u32[]{:S(2)}, u32[]{:S(2)}) collective-permute-start(bf16[2,2,512,128]{3,2,1,0:T(8,128)(2,1)} %get-tuple-element.54), channel_id=1, source_target_pairs={{0,2},{1,3},{2,0},{3,1},{4,6},{5,7},{6,4},{7,5}} | collective-permute-start | bytes 1572872 | tf_op jit(solution)/shard_map/ppermute | solution.py:224
  453.6 17.9 %collective-permute-start.18 = (bf16[2,1,512,128]{3,2,1,0:T(8,128)(2,1)S(1)}, bf16[2,1,512,128]{3,2,1,0:T(8,128)(2,1)S(1)}, u32[]{:S(2)}, u32[]{:S(2)}) collective-permute-start(bf16[2,1,512,128]{3,2,1,0:T(8,128)(2,1)S(1)} %shard_map.90), channel_id=1, source_target_pairs={{0,2},{1,3},{2,0},{3,1},{4,6},{5,7},{6,4},{7,5}} | collective-permute-start | bytes 786440 | tf_op jit(solution)/shard_map/ppermute | solution.py:224
  471.5 14.0 %collective-permute-start.8 = (bf16[2,2,512,128]{3,2,1,0:T(8,128)(2,1)S(1)}, bf16[2,2,512,128]{3,2,1,0:T(8,128)(2,1)S(1)}, u32[]{:S(2)}, u32[]{:S(2)}) collective-permute-start(bf16[2,2,512,128]{3,2,1,0:T(8,128)(2,1)S(1)} %copy-done.13), channel_id=1, source_target_pairs={{0,3},{1,2},{2,1},{3,0},{4,7},{5,6},{6,5},{7,4}} | collective-permute-start | bytes 1572872 | tf_op jit(solution)/shard_map/ppermute | solution.py:224
  477.5 30.8 %collective-permute-start.15 = (bf16[2,4,512,128]{3,2,1,0:T(8,128)(2,1)}, bf16[2,4,512,128]{3,2,1,0:T(8,128)(2,1)S(1)}, u32[]{:S(2)}, u32[]{:S(2)}) collective-permute-start(bf16[2,4,512,128]{3,2,1,0:T(8,128)(2,1)} %get-tuple-element.62), channel_id=1, source_target_pairs={{0,2},{1,3},{2,0},{3,1},{4,6},{5,7},{6,4},{7,5}} | collective-permute-start | bytes 3145736 | tf_op jit(solution)/shard_map/ppermute | solution.py:224
  485.5 46.5 %copy-start.7 = (bf16[2,2,512,128]{3,2,1,0:T(8,128)(2,1)}, bf16[2,2,512,128]{3,2,1,0:T(8,128)(2,1)S(1)}, u32[]{:S(2)}) copy-start(bf16[2,2,512,128]{3,2,1,0:T(8,128)(2,1)S(1)} %collective-permute-done.8.refs_3_) | copy-start | bytes 1572868
  485.5 1.9 collective-permute-start.9
  487.4 43.0 %collective-permute-start.16 = (bf16[2,4,512,128]{3,2,1,0:T(8,128)(2,1)}, bf16[2,4,512,128]{3,2,1,0:T(8,128)(2,1)S(1)}, u32[]{:S(2)}, u32[]{:S(2)}) collective-permute-start(bf16[2,4,512,128]{3,2,1,0:T(8,128)(2,1)} %get-tuple-element.63), channel_id=1, source_target_pairs={{0,3},{1,2},{2,1},{3,0},{4,7},{5,6},{6,5},{7,4}} | collective-permute-start | bytes 3145736 | tf_op jit(solution)/shard_map/ppermute | solution.py:224
  508.3 27.1 %copy-start.3 = (bf16[2,4,512,128]{3,2,1,0:T(8,128)(2,1)}, bf16[2,4,512,128]{3,2,1,0:T(8,128)(2,1)S(1)}, u32[]{:S(2)}) copy-start(bf16[2,4,512,128]{3,2,1,0:T(8,128)(2,1)S(1)} %collective-permute-done.15.refs_2_) | copy-start | bytes 3145732
  508.3 23.6 %collective-permute-start.17 = (bf16[2,4,512,128]{3,2,1,0:T(8,128)(2,1)}, bf16[2,4,512,128]{3,2,1,0:T(8,128)(2,1)S(1)}, u32[]{:S(2)}, u32[]{:S(2)}) collective-permute-start(bf16[2,4,512,128]{3,2,1,0:T(8,128)(2,1)} %get-tuple-element.64), channel_id=1, source_target_pairs={{0,1},{1,0},{2,3},{3,2},{4,5},{5,4},{6,7},{7,6}} | collective-permute-start | bytes 3145736 | tf_op jit(solution)/shard_map/ppermute | solution.py:224
  530.5 116.2 %collective-permute-start.10 = (bf16[2,20,512,128]{3,2,1,0:T(8,128)(2,1)}, bf16[2,20,512,128]{3,2,1,0:T(8,128)(2,1)}, u32[]{:S(2)}, u32[]{:S(2)}) collective-permute-start(bf16[2,20,512,128]{3,2,1,0:T(8,128)(2,1)} %get-tuple-element.57), channel_id=1, source_target_pairs={{0,2},{1,3},{2,0},{3,1},{4,6},{5,7},{6,4},{7,5}} | collective-permute-start | bytes 15728648 | tf_op jit(solution)/shard_map/ppermute | solution.py:224
  532.0 226.1 %collective-permute-start.11 = (bf16[2,20,512,128]{3,2,1,0:T(8,128)(2,1)}, bf16[2,20,512,128]{3,2,1,0:T(8,128)(2,1)}, u32[]{:S(2)}, u32[]{:S(2)}) collective-permute-start(bf16[2,20,512,128]{3,2,1,0:T(8,128)(2,1)} %get-tuple-element.58), channel_id=1, source_target_pairs={{0,3},{1,2},{2,1},{3,0},{4,7},{5,6},{6,5},{7,4}} | collective-permute-start | bytes 15728648 | tf_op jit(solution)/shard_map/ppermute | solution.py:224
  533.0 230.1 %copy-start.2 = (bf16[64,8,128]{2,1,0:T(8,128)(2,1)S(1)}, bf16[64,8,128]{2,1,0:T(8,128)(2,1)}, u32[]{:S(2)}) copy-start(bf16[64,8,128]{2,1,0:T(8,128)(2,1)} %get-tuple-element.44) | copy-start | bytes 393220
  533.0 227.0 %collective-permute-start.12 = (bf16[2,20,512,128]{3,2,1,0:T(8,128)(2,1)}, bf16[2,20,512,128]{3,2,1,0:T(8,128)(2,1)}, u32[]{:S(2)}, u32[]{:S(2)}) collective-permute-start(bf16[2,20,512,128]{3,2,1,0:T(8,128)(2,1)} %get-tuple-element.59), channel_id=1, source_target_pairs={{0,1},{1,0},{2,3},{3,2},{4,5},{5,4},{6,7},{7,6}} | collective-permute-start | bytes 15728648 | tf_op jit(solution)/shard_map/ppermute | solution.py:224
  646.7 115.8 %collective-permute-start.4 = (bf16[2,1,352,128]{3,2,1,0:T(8,128)(2,1)}, bf16[2,1,352,128]{3,2,1,0:T(8,128)(2,1)S(1)}, u32[]{:S(2)}, u32[]{:S(2)}) collective-permute-start(bf16[2,1,352,128]{3,2,1,0:T(8,128)(2,1)} %get-tuple-element.50), channel_id=1, source_target_pairs={{0,2},{1,3},{2,0},{3,1},{4,6},{5,7},{6,4},{7,5}} | collective-permute-start | bytes 540680 | tf_op jit(solution)/shard_map/ppermute | solution.py:224
  758.1 72.1 %collective-permute-start.5 = (bf16[2,1,352,128]{3,2,1,0:T(8,128)(2,1)}, bf16[2,1,352,128]{3,2,1,0:T(8,128)(2,1)}, u32[]{:S(2)}, u32[]{:S(2)}) collective-permute-start(bf16[2,1,352,128]{3,2,1,0:T(8,128)(2,1)} %get-tuple-element.51), channel_id=1, source_target_pairs={{0,3},{1,2},{2,1},{3,0},{4,7},{5,6},{6,5},{7,4}} | collective-permute-start | bytes 540680 | tf_op jit(solution)/shard_map/ppermute | solution.py:224
  760.0 70.2 %collective-permute-start.6 = (bf16[2,1,352,128]{3,2,1,0:T(8,128)(2,1)}, bf16[2,1,352,128]{3,2,1,0:T(8,128)(2,1)}, u32[]{:S(2)}, u32[]{:S(2)}) collective-permute-start(bf16[2,1,352,128]{3,2,1,0:T(8,128)(2,1)} %get-tuple-element.52), channel_id=1, source_target_pairs={{0,1},{1,0},{2,3},{3,2},{4,5},{5,4},{6,7},{7,6}} | collective-permute-start | bytes 540680 | tf_op jit(solution)/shard_map/ppermute | solution.py:224
  760.0 72.3 %collective-permute-start.1 = (bf16[2,1,160,128]{3,2,1,0:T(8,128)(2,1)}, bf16[2,1,160,128]{3,2,1,0:T(8,128)(2,1)}, u32[]{:S(2)}, u32[]{:S(2)}) collective-permute-start(bf16[2,1,160,128]{3,2,1,0:T(8,128)(2,1)} %get-tuple-element.46), channel_id=1, source_target_pairs={{0,2},{1,3},{2,0},{3,1},{4,6},{5,7},{6,4},{7,5}} | collective-permute-start | bytes 245768 | tf_op jit(solution)/shard_map/ppermute | solution.py:224
  760.5 71.7 %collective-permute-start.2 = (bf16[2,1,160,128]{3,2,1,0:T(8,128)(2,1)}, bf16[2,1,160,128]{3,2,1,0:T(8,128)(2,1)}, u32[]{:S(2)}, u32[]{:S(2)}) collective-permute-start(bf16[2,1,160,128]{3,2,1,0:T(8,128)(2,1)} %get-tuple-element.47), channel_id=1, source_target_pairs={{0,3},{1,2},{2,1},{3,0},{4,7},{5,6},{6,5},{7,4}} | collective-permute-start | bytes 245768 | tf_op jit(solution)/shard_map/ppermute | solution.py:224
  763.1 69.2 %collective-permute-start.3 = (bf16[2,1,160,128]{3,2,1,0:T(8,128)(2,1)}, bf16[2,1,160,128]{3,2,1,0:T(8,128)(2,1)}, u32[]{:S(2)}, u32[]{:S(2)}) collective-permute-start(bf16[2,1,160,128]{3,2,1,0:T(8,128)(2,1)} %get-tuple-element.48), channel_id=1, source_target_pairs={{0,1},{1,0},{2,3},{3,2},{4,5},{5,4},{6,7},{7,6}} | collective-permute-start | bytes 245768 | tf_op jit(solution)/shard_map/ppermute | solution.py:224
  (11 other events, 97.7 us)
